TPU v7x, 32 devices: a whole 2x2x4 slice. The times are simulated.
32 devices in a mesh: slab: 8 (over z, y), sub: 4 (over x, core).
Axes of the slice: x: 2, y: 2, z: 4, core: 2. Of those that a mesh axis runs over, the one named last changes fastest.
Arguments:
- right_side: float32 [16, 8, 1, 16, 128], P('slab', 'sub'), may hold values from -8 to 8
- blocks: float32 [16, 8, 1, 7, 128, 128], P('slab', 'sub'), may hold values from -2300 to 4500, as said below
- pattern: int32 [16, 8, 1, 7], P('slab', 'sub'), may hold values from 0 to 127, as said below
- aggregates: int32 [16, 8, 1, 128], P('slab', 'sub'), may hold values from 0 to 127
- coarse_inverse: float32 [1024, 1024], P(('slab', 'sub')), may hold values from -0.1 to 0.8, as said below
Outputs:
- solution: float32 [16, 8, 1, 16, 128], P('slab', 'sub')
- residual: float32 [16, 8, 1, 16, 128], P('slab', 'sub')
Inputs may be any that keep to these rules, and one draw needn't show every extreme that they name: `blocks`: taken with pattern, the operator A is symmetric positive definite, and the line systems of the steps are diagonally dominant with positive diagonals. `pattern`: the 7 entries of block row b list, in some order, b itself and the numbers of its six neighbours along x, y and z; a neighbour outside the grid of 16 x 8 x 1 block is replaced by b itself. `coarse_inverse`: symmetric positive definite.
All inputs are finite; a program needn't handle non-finite values.
Results may differ from a plain program's by a relative error of at most 0.0003.
Values sent between devices are 32-bit elements; how exact they have to be, the bound alone decides.
A program may use at most 128 MiB of HBM per device.

v0:
```python
import jax
import jax.numpy as jnp
from jax import lax
from jax.sharding import PartitionSpec as P

HIGHEST = lax.Precision.HIGHEST


def padded_2(x, sides, width):
    for axis, dim in sides:
        size, length = (lax.axis_size(axis), x.shape[dim])
        up = [(i, (i + 1) % size) for i in range(size - 1)]
        down = [(j, i) for i, j in up]
        last = lax.slice_in_dim(x, length - width, length, axis=dim)
        leading = lax.slice_in_dim(x, 0, width, axis=dim)
        before = lax.ppermute(last, axis, up)
        after = lax.ppermute(leading, axis, down)
        x = jnp.concatenate([before, x, after], axis=dim)
    return x


def prefix_2(value, axis, join, neutral, backward):
    count, mine = (lax.axis_size(axis), lax.axis_index(axis))
    pieces = jax.tree.map(lambda part: lax.all_gather(part, axis), value)
    if backward:
        pieces = jax.tree.map(lambda part: part[::-1], pieces)
        mine = count - 1 - mine
    subtotal = jax.tree.map(
        lambda part, zero: jnp.full_like(part, 0) + jnp.asarray(zero, part.dtype), value, neutral
    )

    def lap(position, subtotal):
        longer = join(subtotal, jax.tree.map(lambda part: part[position], pieces))
        return jax.tree.map(lambda new, old: jnp.where(position < mine, new, old), longer, subtotal)

    return lax.fori_loop(0, count - 1, lap, subtotal)


def passed_along(value, axis, steps):
    count = lax.axis_size(axis)
    leading, last = (max(0, -steps), min(count, count - steps))
    return lax.ppermute(value, axis, [(source, source + steps) for source in range(leading, last)])


def compose(earlier, later):
    return (later[0] * earlier[0], later[0][:, :, None, :] * earlier[1] + later[1])


def mobius(earlier, later):
    top_left = later[0] * earlier[0] + later[1] * earlier[2]
    top_right = later[0] * earlier[1] + later[1] * earlier[3]
    low_left = later[2] * earlier[0] + later[3] * earlier[2]
    low_right = later[2] * earlier[1] + later[3] * earlier[3]
    scale = jnp.maximum(
        jnp.maximum(jnp.abs(top_left), jnp.abs(top_right)),
        jnp.maximum(jnp.abs(low_left), jnp.abs(low_right)),
    )
    return (top_left / scale, top_right / scale, low_left / scale, low_right / scale)


def per_device(right_side, blocks, pattern, aggregates, coarse_inverse):
    depth_count, cross_count, side_count, rhs_count, cell_count = right_side.shape
    slot_count = pattern.shape[-1]
    block_rows = depth_count * cross_count * side_count
    slab_index = lax.axis_index("slab")
    sub_index = lax.axis_index("sub")
    global_cross = cross_count * lax.axis_size("sub")
    plane_blocks = global_cross * side_count
    z_position = slab_index * depth_count + lax.iota(jnp.int32, depth_count)
    x_position = sub_index * cross_count + lax.iota(jnp.int32, cross_count)
    y_position = lax.iota(jnp.int32, side_count)
    own_number = (
        z_position[:, None, None] * global_cross + x_position[None, :, None]
    ) * side_count + y_position[None, None, :]
    diagonals = jnp.diagonal(blocks, axis1=-2, axis2=-1)
    is_self = (pattern == own_number[..., None]).astype(jnp.float32)
    is_below = (pattern == (own_number - plane_blocks)[..., None]).astype(jnp.float32)
    line_diagonal = jnp.sum(diagonals * is_self[..., None], axis=3)
    line_coupling = jnp.sum(diagonals * is_below[..., None], axis=3)
    plane_number = pattern // plane_blocks
    remain = pattern % plane_blocks
    local_plane = plane_number - slab_index * depth_count + 1
    local_cross = remain // side_count - sub_index * cross_count + 1
    local_index = (
        (local_plane * (cross_count + 2) + local_cross) * side_count + remain % side_count
    ).reshape(block_rows, slot_count)
    flat_blocks = blocks.reshape(block_rows, slot_count, cell_count, cell_count)

    def operator_apply(vector):
        padded = padded_2(vector, (("slab", 0), ("sub", 1)), 1)
        nearby = padded.reshape(-1, rhs_count, cell_count)[local_index]
        product = jnp.einsum(
            "rsij,rskj->rki",
            flat_blocks,
            nearby,
            precision=HIGHEST,
            preferred_element_type=jnp.float32,
        )
        return product.reshape(right_side.shape)

    line_shape = line_diagonal.shape[1:]
    unit_gain = jnp.ones(line_shape, jnp.float32)
    zero_line = jnp.zeros(line_shape, jnp.float32)
    element = (unit_gain, zero_line, zero_line, unit_gain)
    for height in range(depth_count):
        squared = line_coupling[height] * line_coupling[height]
        element = mobius(element, (line_diagonal[height], -squared, unit_gain, zero_line))
    prefix = prefix_2(element, "slab", mobius, (unit_gain, zero_line, zero_line, unit_gain), False)
    leading = prefix[0]
    trailing = prefix[2]
    pivot_rows = []
    for height in range(depth_count):
        squared = line_coupling[height] * line_coupling[height]
        pivot = (line_diagonal[height] * leading - squared * trailing) / leading
        pivot_rows.append(pivot)
        leading = pivot
        trailing = unit_gain
    pivots = jnp.stack(pivot_rows)
    coupling_above = passed_along(line_coupling[0], "slab", -1)
    upper_coupling = jnp.concatenate([line_coupling[1:], coupling_above[None]], axis=0)
    forward_factor = -line_coupling / pivots
    backward_factor = -upper_coupling / pivots
    inverse_pivot = 1.0 / pivots
    zero_offset = jnp.zeros(right_side.shape[1:], jnp.float32)

    def line_solve(vector):
        scaled = vector * inverse_pivot[:, :, :, None, :]
        factor, offset = (unit_gain, zero_offset)
        for height in range(depth_count):
            factor, offset = compose((factor, offset), (forward_factor[height], scaled[height]))
        before = prefix_2((factor, offset), "slab", compose, (unit_gain, zero_offset), False)
        carried = before[1]
        forward_rows = []
        for height in range(depth_count):
            carried = forward_factor[height][:, :, None, :] * carried + scaled[height]
            forward_rows.append(carried)
        factor, offset = (unit_gain, zero_offset)
        for height in reversed(range(depth_count)):
            factor, offset = compose(
                (factor, offset), (backward_factor[height], forward_rows[height])
            )
        beyond = prefix_2((factor, offset), "slab", compose, (unit_gain, zero_offset), True)
        carried = beyond[1]
        solved_rows = [zero_offset] * depth_count
        for height in reversed(range(depth_count)):
            carried = backward_factor[height][:, :, None, :] * carried + forward_rows[height]
            solved_rows[height] = carried
        return jnp.stack(solved_rows)

    owned_rows = coarse_inverse.shape[0]
    layer_aggregates = owned_rows * lax.axis_size("sub")
    onehot = (
        aggregates.reshape(block_rows, 1, cell_count)
        == lax.iota(jnp.int32, layer_aggregates)[None, :, None]
    ).astype(jnp.float32)

    def fold_rows(piece):
        return jnp.dot(coarse_inverse, piece, precision=HIGHEST, preferred_element_type=jnp.float32)

    def coarse_apply(vector):
        local_sums = jnp.einsum(
            "rac,rkc->ak",
            onehot,
            vector.reshape(block_rows, rhs_count, cell_count),
            precision=HIGHEST,
            preferred_element_type=jnp.float32,
        )
        layer_total = lax.psum(local_sums, "sub")
        owned_values = fold_rows(lax.all_gather(layer_total, "slab", axis=0, tiled=True))
        layer_values = lax.all_gather(owned_values, "sub", axis=0, tiled=True)
        spread = jnp.einsum(
            "rac,ak->rkc",
            onehot,
            layer_values,
            precision=HIGHEST,
            preferred_element_type=jnp.float32,
        )
        return spread.reshape(right_side.shape)

    def precondition(vector):
        return line_solve(vector) + coarse_apply(vector)

    def local_inner(left, right):
        return jnp.sum(left * right, axis=(0, 1, 2, 4))

    solution = jnp.zeros_like(right_side)
    residual = right_side

    def paired(vector_r, vector_z, vector_w):
        return lax.psum(
            (local_inner(vector_r, vector_z), local_inner(vector_w, vector_z)), ("slab", "sub")
        )

    smoothed = precondition(residual)
    applied = operator_apply(smoothed)
    energy, curvature = paired(residual, smoothed, applied)
    step_length = energy / curvature
    direction = smoothed
    along = applied
    solution = solution + step_length[:, None] * direction
    residual = residual - step_length[:, None] * along
    smoothed = precondition(residual)
    applied = operator_apply(smoothed)
    energy_next, curvature = paired(residual, smoothed, applied)
    growth = energy_next / energy
    step_length = energy_next / (curvature - growth * energy_next / step_length)
    direction = smoothed + growth[:, None] * direction
    along = applied + growth[:, None] * along
    solution = solution + step_length[:, None] * direction
    residual = residual - step_length[:, None] * along
    return (solution, residual)


def solution(mesh):
    placed = (
        P("slab", "sub", None, None, None),
        P("slab", "sub", None, None, None, None),
        P("slab", "sub", None, None),
        P("slab", "sub", None, None),
        P(("slab", "sub"), None),
    )
    return jax.shard_map(
        per_device,
        mesh=mesh,
        in_specs=placed,
        out_specs=(P("slab", "sub", None, None, None), P("slab", "sub", None, None, None)),
        check_vma=False,
    )
```

profile of v0, /device:TPU:0, one launch (start us, length us, event | category | flops | bytes accessed | tf_op | source)
XLA Modules:
  0.0 465.3 jit_solution(13437016449610730045)
XLA Ops:
  0.7 25.1 %copy.208 = f32[2,2,1,7,128,128]{3,1,5,4,0,2:T(2,128)} copy(f32[2,2,1,7,128,128]{5,4,3,2,1,0:T(8,128)} %param.16) | data formatting | bytes 3670016 | tf_op args[1]
  25.9 2.0 gather_fusion
  28.0 0.9 fusion.5
  28.9 1.3 collective-permute-start
  30.6 23.4 %all_gather.60 = f32[8,2,1,128]{3,1,2,0:T(2,128)S(1)} all-gather(f32[1,2,1,128]{3,1,2,0:T(2,128)S(1)} %get-tuple-element.815), channel_id=1, replica_groups=mesh['slab'=8,'sub'=4] {'slab'}, dimensions={0}, use_global_device_ids=true | all-gather | bytes 9216 | tf_op jit(solution)/shard_map/all_gather | solution.py:24
  54.0 16.3 %all_gather.61 = f32[8,2,1,128]{3,1,2,0:T(2,128)S(1)} all-gather(f32[1,2,1,128]{3,1,2,0:T(2,128)S(1)} %get-tuple-element.814), channel_id=1, replica_groups=mesh['slab'=8,'sub'=4] {'slab'}, dimensions={0}, use_global_device_ids=true | all-gather | bytes 9216 | tf_op jit(solution)/shard_map/all_gather | solution.py:24
  70.3 18.3 %all_gather.62 = f32[8,2,1,128]{3,1,2,0:T(2,128)S(1)} all-gather(f32[1,2,1,128]{3,1,2,0:T(2,128)S(1)} %get-tuple-element.816), channel_id=1, replica_groups=mesh['slab'=8,'sub'=4] {'slab'}, dimensions={0}, use_global_device_ids=true | all-gather | bytes 9216 | tf_op jit(solution)/shard_map/all_gather | solution.py:24
  88.6 16.3 %all_gather.63 = f32[8,2,1,128]{3,1,2,0:T(2,128)S(1)} all-gather(f32[1,2,1,128]{3,1,2,0:T(2,128)S(1)} %get-tuple-element.789), channel_id=1, replica_groups=mesh['slab'=8,'sub'=4] {'slab'}, dimensions={0}, use_global_device_ids=true | all-gather | bytes 9216 | tf_op jit(solution)/shard_map/all_gather | solution.py:24
  104.9 0.8 while.76
  105.9 5.9 %psum.42 = f32[128,16]{0,1:T(8,128)S(1)} all-reduce(f32[128,16]{0,1:T(8,128)S(1)} %convolution_bitcast_fusion.3), channel_id=1, replica_groups=mesh['slab'=8,'sub'=4] {'sub'}, use_global_device_ids=true, to_apply=%region_8.9 | all-reduce | flops 2048 | bytes 16384 | tf_op jit(solution)/shard_map/psum | solution.py:168
  111.9 30.5 %all_gather.69 = f32[1024,16]{0,1:T(8,128)S(1)} all-gather(f32[128,16]{0,1:T(8,128)S(1)} %psum.42), channel_id=1, replica_groups=mesh['slab'=8,'sub'=4] {'slab'}, dimensions={0}, use_global_device_ids=true | all-gather | bytes 73728 | tf_op jit(solution)/shard_map/all_gather | solution.py:169
  142.4 0.2 convolution_bitcast_fusion.2
  142.6 5.2 %all-gather.2 = f32[4,32,16]{1,2,0:T(8,128)S(1)} all-gather(f32[1,32,16]{1,2,0:T(8,128)S(1)} %convolution_bitcast_fusion.2), channel_id=1, replica_groups=mesh['slab'=8,'sub'=4] {'sub'}, dimensions={0}, use_global_device_ids=true | all-gather | bytes 10240 | tf_op jit(solution)/shard_map/all_gather | solution.py:170
  147.9 0.2 fusion.7
  148.3 30.5 %all_gather.66 = f32[8,2,1,16,128]{4,3,2,1,0:T(8,128)S(1)} all-gather(f32[1,2,1,16,128]{4,3,2,1,0:T(8,128)S(1)} %bitcast_add_fusion.10), channel_id=1, replica_groups=mesh['slab'=8,'sub'=4] {'slab'}, dimensions={0}, use_global_device_ids=true | all-gather | bytes 147456 | tf_op jit(solution)/shard_map/all_gather | solution.py:24
  178.8 18.3 %all_gather.65 = f32[8,2,1,128]{3,1,2,0:T(2,128)S(1)} all-gather(f32[1,2,1,128]{3,1,2,0:T(2,128)S(1)} %get-tuple-element.821), channel_id=1, replica_groups=mesh['slab'=8,'sub'=4] {'slab'}, dimensions={0}, use_global_device_ids=true | all-gather | bytes 9216 | tf_op jit(solution)/shard_map/all_gather | solution.py:24
  197.1 0.3 while.77
  197.4 30.5 %all-gather = f32[16,1,16,128]{3,2,1,0:T(8,128)S(1)} all-gather(f32[2,1,16,128]{3,2,1,0:T(8,128)S(1)} %get-tuple-element.785), channel_id=2, replica_groups=mesh['slab'=8,'sub'=4] {'slab'}, dimensions={0}, use_global_device_ids=true | all-gather | bytes 147456 | tf_op jit(solution)/shard_map/all_gather | solution.py:24
  228.0 16.3 %all_gather.64 = f32[8,2,1,128]{3,1,2,0:T(2,128)S(1)} all-gather(f32[1,2,1,128]{3,1,2,0:T(2,128)S(1)} %get-tuple-element.818), channel_id=1, replica_groups=mesh['slab'=8,'sub'=4] {'slab'}, dimensions={0}, use_global_device_ids=true | all-gather | bytes 9216 | tf_op jit(solution)/shard_map/all_gather | solution.py:24
  244.3 0.3 while.78
  244.8 3.9 collective-permute-start.1
  248.7 1.3 collective-permute-start.2
  250.1 4.2 collective-permute-done.2
  254.4 1.3 collective-permute-start.3
  255.7 1.3 collective-permute-start.4
  257.0 3.7 collective-permute-done.4
  260.8 0.6 gather_fusion.1
  261.4 1.9 fusion.15
  263.3 38.8 %all-reduce.1 = (f32[16]{0:T(128)S(1)}, f32[16]{0:T(128)S(1)}) all-reduce(f32[16]{0:T(128)S(1)} %get-tuple-element.783, f32[16]{0:T(128)S(1)} %get-tuple-element.833), channel_id=1, replica_groups=mesh['slab'=8,'sub'=4] {'slab','sub'}, use_global_device_ids=true, to_apply=%region_10.11 | all-reduce | flops 32 | bytes 256 | tf_op jit(solution)/shard_map/psum | solution.py:190
  302.1 30.5 %all_gather.71 = f32[8,2,1,16,128]{4,3,2,1,0:T(8,128)S(1)} all-gather(f32[1,2,1,16,128]{4,3,2,1,0:T(8,128)S(1)} %add_bitcast_fusion.3), channel_id=1, replica_groups=mesh['slab'=8,'sub'=4] {'slab'}, dimensions={0}, use_global_device_ids=true | all-gather | bytes 147456 | tf_op jit(solution)/shard_map/all_gather | solution.py:24
  332.7 0.3 while.79
  333.0 30.5 %all-gather.1 = f32[16,1,16,128]{3,2,1,0:T(8,128)S(1)} all-gather(f32[2,1,16,128]{3,2,1,0:T(8,128)S(1)} %get-tuple-element.779), channel_id=3, replica_groups=mesh['slab'=8,'sub'=4] {'slab'}, dimensions={0}, use_global_device_ids=true | all-gather | bytes 147456 | tf_op jit(solution)/shard_map/all_gather | solution.py:24
  363.6 0.4 while.80
  364.1 6.1 %psum.45 = f32[128,16]{0,1:T(8,128)S(1)} all-reduce(f32[128,16]{0,1:T(8,128)S(1)} %convolution_bitcast_fusion.1), channel_id=1, replica_groups=mesh['slab'=8,'sub'=4] {'sub'}, use_global_device_ids=true, to_apply=%region_17.18 | all-reduce | flops 2048 | bytes 16384 | tf_op jit(solution)/shard_map/psum | solution.py:168
  370.2 30.5 %all_gather.74 = f32[1024,16]{0,1:T(8,128)S(1)} all-gather(f32[128,16]{0,1:T(8,128)S(1)} %psum.45), channel_id=1, replica_groups=mesh['slab'=8,'sub'=4] {'slab'}, dimensions={0}, use_global_device_ids=true | all-gather | bytes 73728 | tf_op jit(solution)/shard_map/all_gather | solution.py:169
  400.8 0.2 convolution_bitcast_fusion
  401.0 5.5 %all-gather.3 = f32[4,32,16]{1,2,0:T(8,128)S(1)} all-gather(f32[1,32,16]{1,2,0:T(8,128)S(1)} %convolution_bitcast_fusion), channel_id=1, replica_groups=mesh['slab'=8,'sub'=4] {'sub'}, dimensions={0}, use_global_device_ids=true | all-gather | bytes 10240 | tf_op jit(solution)/shard_map/all_gather | solution.py:170
  406.6 0.2 fusion.6
  406.9 2.5 collective-permute-start.5
  409.5 1.3 collective-permute-start.6
  410.9 4.2 collective-permute-done.6
  415.1 1.3 collective-permute-start.7
  416.4 1.3 collective-permute-start.8
  417.8 2.8 collective-permute-done.8
  420.6 0.6 gather_fusion.2
  421.1 1.9 fusion.13
  423.1 41.5 %all-reduce = (f32[16]{0:T(128)S(1)}, f32[16]{0:T(128)S(1)}) all-reduce(f32[16]{0:T(128)S(1)} %get-tuple-element.777, f32[16]{0:T(128)S(1)} %get-tuple-element.835), channel_id=1, replica_groups=mesh['slab'=8,'sub'=4] {'slab','sub'}, use_global_device_ids=true, to_apply=%region_19.20 | all-reduce | flops 32 | bytes 256 | tf_op jit(solution)/shard_map/psum | solution.py:190
  464.6 0.7 subtract_bitcast_fusion
  (166 shorter events, 2.8 us)
Async XLA Ops:
  0.6 141.8 %copy-start = (f32[32,1024]{1,0:T(8,128)S(1)}, f32[32,1024]{1,0:T(8,128)}, u32[]{:S(2)}) copy-start(f32[32,1024]{1,0:T(8,128)} %param.19) | copy-start | bytes 393220
  0.7 27.2 %copy-start.3 = (s32[2,2,1,7]{3,2,1,0:T(1,128)S(1)}, s32[2,2,1,7]{3,2,1,0:T(1,128)}, u32[]{:S(2)}) copy-start(s32[2,2,1,7]{3,2,1,0:T(1,128)} %param.17) | copy-start | bytes 340
  0.7 105.0 %copy-start.2 = (f32[2,2,1,16,128]{4,3,2,1,0:T(8,128)S(1)}, f32[2,2,1,16,128]{4,3,2,1,0:T(8,128)}, u32[]{:S(2)}) copy-start(f32[2,2,1,16,128]{4,3,2,1,0:T(8,128)} %param.15) | copy-start | bytes 98308
  25.8 80.0 %copy-start.4 = (s32[2,2,1,128]{3,2,1,0:T(1,128)S(1)}, s32[2,2,1,128]{3,2,1,0:T(1,128)}, u32[]{:S(2)}) copy-start(s32[2,2,1,128]{3,2,1,0:T(1,128)} %param.18) | copy-start | bytes 6148
  28.9 119.2 %collective-permute-start = (f32[2,1,128]{2,0,1:T(2,128)S(1)}, f32[2,1,128]{2,0,1:T(2,128)S(1)}, u32[]{:S(2)}, u32[]{:S(2)}) collective-permute-start(f32[2,1,128]{2,0,1:T(2,128)S(1)} %get-tuple-element.826), channel_id=1, source_target_pairs={{4,0},{8,4},{12,8},{16,12},{20,16},{24,20},{28,24},{5,1},{9,5},{13... | collective-permute-start | bytes 3080 | tf_op jit(solution)/shard_map/ppermute | solution.py:42
  105.7 155.6 %copy-start.1 = (f32[2,2,1,7,128,128]{5,4,3,2,1,0:T(8,128)S(1)}, f32[2,2,1,7,128,128]{5,4,3,2,1,0:T(8,128)}, u32[]{:S(2)}) copy-start(f32[2,2,1,7,128,128]{5,4,3,2,1,0:T(8,128)} %param.16) | copy-start | bytes 5505028
  244.8 5.4 %collective-permute-start.1 = (f32[1,2,1,16,128]{4,3,1,2,0:T(8,128)S(1)}, f32[1,2,1,16,128]{4,3,1,2,0:T(8,128)S(1)}, u32[]{:S(2)}, u32[]{:S(2)}) collective-permute-start(f32[1,2,1,16,128]{4,3,1,2,0:T(8,128)S(1)} %get-tuple-element.812), channel_id=1, source_target_pairs={{0,4},{4,8},{8,12},{12,16},{16,20},{20,24},{24,28},{1,5},{5,9},{9,... | collective-permute-start | bytes 49160 | tf_op jit(solution)/shard_map/ppermute | solution.py:16
  248.7 5.6 %collective-permute-start.2 = (f32[1,2,1,16,128]{4,3,1,2,0:T(8,128)S(1)}, f32[1,2,1,16,128]{4,3,1,2,0:T(8,128)S(1)}, u32[]{:S(2)}, u32[]{:S(2)}) collective-permute-start(f32[1,2,1,16,128]{4,3,1,2,0:T(8,128)S(1)} %get-tuple-element.813), channel_id=1, source_target_pairs={{4,0},{8,4},{12,8},{16,12},{20,16},{24,20},{28,24},{5,1},{9,5},{13... | collective-permute-start | bytes 49160 | tf_op jit(solution)/shard_map/ppermute | solution.py:17
  254.4 2.6 collective-permute-start.3
  255.7 5.1 %collective-permute-start.4 = (f32[4,1,1,16,128]{4,3,1,2,0:T(8,128)S(1)}, f32[4,1,1,16,128]{4,3,1,2,0:T(8,128)S(1)}, u32[]{:S(2)}, u32[]{:S(2)}) collective-permute-start(f32[4,1,1,16,128]{4,3,1,2,0:T(8,128)S(1)} %get-tuple-element.807), channel_id=1, source_target_pairs={{1,0},{2,1},{3,2},{5,4},{6,5},{7,6},{9,8},{10,9},{11,10},{13,12},{... | collective-permute-start | bytes 98312 | tf_op jit(solution)/shard_map/ppermute | solution.py:17
  406.9 4.0 collective-permute-start.5
  409.5 5.6 %collective-permute-start.6 = (f32[1,2,1,16,128]{4,3,1,2,0:T(8,128)S(1)}, f32[1,2,1,16,128]{4,3,1,2,0:T(8,128)S(1)}, u32[]{:S(2)}, u32[]{:S(2)}) collective-permute-start(f32[1,2,1,16,128]{4,3,1,2,0:T(8,128)S(1)} %get-tuple-element.809), channel_id=1, source_target_pairs={{4,0},{8,4},{12,8},{16,12},{20,16},{24,20},{28,24},{5,1},{9,5},{13... | collective-permute-start | bytes 49160 | tf_op jit(solution)/shard_map/ppermute | solution.py:17
  415.1 2.6 collective-permute-start.7
  416.4 4.1 collective-permute-start.8
where the time goes:
time: 468 us; the launch traced here: 465 us
  blocking collectives  395 us (84%)
  local copies, waits for them, and re-layouts  29.3 us (6%)
  starting transfers between devices  15.5 us (3%)
  waiting for transfers between devices  15.1 us (3%)
  matrix products  4.95 us (1%)
    all_gather x10, blocking collectives, prefix_2(): pieces = jax.tree.map(lambda part: lax.all_gather(part, axis), value)  231 us
    psum x2, blocking collectives, paired(): lax.psum((local_inner(vector_r, vector_z), local_inner(vector_w, vector_z...  80.3 us
    all_gather x2, blocking collectives, coarse_apply(): lax.all_gather(layer_total, 'slab', axis=0, tiled=True)  61.1 us
    unnamed x15, local copies, waits for them, and re-layouts  25.4 us
    ppermute x4, waiting for transfers between devices, padded_2(): after = lax.ppermute(leading, axis, down)  14.9 us
    psum x2, blocking collectives, coarse_apply(): layer_total = lax.psum(local_sums, 'sub')  12 us
    all_gather x2, blocking collectives, coarse_apply(): layer_values = lax.all_gather(owned_values, 'sub', axis=0, tiled=True)  10.8 us
  transfers between devices with their start and end apart: 9, of which 5 were waited for; matrix products, arithmetic and copies ran while one was open for 0% of the time, Pallas kernels for 0%

commit v1 on v0

v1 whole, which is shorter than its diff:
```python
import functools
import jax
import jax.numpy as jnp
from jax import lax
from jax.experimental import pallas as pl
from jax.experimental.pallas import tpu as pltpu
from jax.sharding import PartitionSpec as P

HIGHEST = lax.Precision.HIGHEST
MESH = pl.DeviceIdType.MESH
F32 = jnp.float32


def dot_nt(left, right):
    return lax.dot_general(
        left, right, (((1,), (1,)), ((), ())), precision=HIGHEST, preferred_element_type=F32
    )


def dot_nn(left, right):
    return lax.dot_general(
        left, right, (((1,), (0,)), ((), ())), precision=HIGHEST, preferred_element_type=F32
    )


def kernel(
    n_slab, n_sub, pattern, rhs, blocks, agg, inverse, sol, res,
    lines_r, lines_w, coefs, factors, solved, sub_a, sub_c, sub_e, slab_a, slab_c, slab_e,
    inv_all, halo_0, halo_1, applied_0, onehot,
    line_send, line_recv, coef_send, coef_recv, inv_send, inv_recv,
    sub_send, sub_recv, slab_send, slab_recv, halo_send, halo_recv,
):
    D, X, S, K, C = rhs.shape
    slots = blocks.shape[3]
    aggregates = inv_all.shape[0] * inv_all.shape[1]
    slab, sub = lax.axis_index("slab"), lax.axis_index("sub")
    cells = [(x, s) for x in range(X) for s in range(S)]
    rows = [(d, x, s) for d in range(D) for x, s in cells]
    width = len(cells)

    barrier = pltpu.get_barrier_semaphore()
    for step in range(1, n_slab):
        pl.semaphore_signal(
            barrier, inc=1, device_id=(lax.rem(slab + step, n_slab), sub), device_id_type=MESH
        )
    for step in range(1, n_sub):
        pl.semaphore_signal(
            barrier, inc=1, device_id=(slab, lax.rem(sub + step, n_sub)), device_id_type=MESH
        )

    def copies(axis, buffer, send, recv, source=None):
        count, mine = (n_slab, slab) if axis == "slab" else (n_sub, sub)
        made = []
        for step in range(1, count):
            peer = lax.rem(mine + step, count)
            target = (peer, sub) if axis == "slab" else (slab, peer)
            made.append(
                pltpu.make_async_remote_copy(
                    src_ref=buffer.at[mine] if source is None else source,
                    dst_ref=buffer.at[mine],
                    send_sem=send.at[step],
                    recv_sem=recv.at[mine],
                    device_id=target,
                    device_id_type=MESH,
                )
            )
        for copy in made:
            copy.start()

        def wait():
            for step in range(1, count):
                peer = lax.rem(mine + step, count)
                pltpu.make_async_remote_copy(
                    src_ref=buffer.at[peer],
                    dst_ref=buffer.at[peer],
                    send_sem=send.at[step],
                    recv_sem=recv.at[peer],
                    device_id=(peer, sub) if axis == "slab" else (slab, peer),
                    device_id_type=MESH,
                ).wait_recv()
            for copy in made:
                copy.wait_send()

        return wait

    a_index = lax.broadcasted_iota(jnp.int32, (aggregates, C), 0)
    for n, (d, x, s) in enumerate(rows):
        onehot[n] = (agg[d, x, s][None, :] == a_index).astype(F32)

    def local_sums(read):
        total = jnp.zeros((K, aggregates), F32)
        for n, (d, x, s) in enumerate(rows):
            total = total + dot_nt(read(d, x, s), onehot[n])
        return total

    sub_a[sub] = local_sums(lambda d, x, s: rhs[d, x, s])
    lines_r[slab] = rhs[...]
    inv_all[sub] = inverse[...]

    global_cross = X * n_sub
    plane_blocks = global_cross * S
    eye = (
        lax.broadcasted_iota(jnp.int32, (C, C), 0) == lax.broadcasted_iota(jnp.int32, (C, C), 1)
    ).astype(F32)
    for n, (d, x, s) in enumerate(rows):
        own = ((slab * D + d) * global_cross + sub * X + x) * S + s
        diagonal = jnp.zeros((C, C), F32)
        coupling = jnp.zeros((C, C), F32)
        for slot in range(slots):
            number = pattern[n * slots + slot]
            block = blocks[d, x, s, slot]
            diagonal = diagonal + (number == own).astype(F32) * block
            coupling = coupling + (number == own - plane_blocks).astype(F32) * block
        coefs[slab, pl.ds(n, 1)] = jnp.sum(diagonal * eye, axis=0, keepdims=True)
        coefs[slab, pl.ds(len(rows) + n, 1)] = jnp.sum(coupling * eye, axis=0, keepdims=True)

    pl.semaphore_wait(barrier, n_slab + n_sub - 2)

    sums_wait = copies("sub", sub_a, sub_send.at[0], sub_recv.at[0])
    coefs_wait = copies("slab", coefs, coef_send, coef_recv)
    lines_wait = copies("slab", lines_r, line_send.at[0], line_recv.at[0], rhs)
    inv_wait = copies("sub", inv_all, inv_send, inv_recv, inverse)

    sums_wait()
    total = sub_a[0]
    for other in range(1, n_sub):
        total = total + sub_a[other]
    slab_a[slab] = total
    slab_wait = copies("slab", slab_a, slab_send.at[0], slab_recv.at[0])

    coefs_wait()
    planes = n_slab * D

    def coef(kind, z):
        start = kind * len(rows) + (z % D) * width
        return coefs[z // D, pl.ds(start, width)]

    pivot = coef(0, 0)
    for z in range(planes):
        if z > 0:
            below = coef(1, z)
            pivot = coef(0, z) - below * below / pivot
        inverse_pivot = 1.0 / pivot
        factors[z, 0] = inverse_pivot
        factors[z, 1] = -coef(1, z) * inverse_pivot
        if z + 1 < planes:
            factors[z, 2] = -coef(1, z + 1) * inverse_pivot

    def line_solve(read):
        carried = [None] * width
        for z in range(planes):
            for w, (x, s) in enumerate(cells):
                value = read(z // D, z % D, x, s) * factors[z, 0, pl.ds(w, 1)]
                if z > 0:
                    value = value + factors[z, 1, pl.ds(w, 1)] * carried[w]
                carried[w] = value
                solved[z, x, s] = value
        for z in reversed(range(planes - 1)):
            for w, (x, s) in enumerate(cells):
                carried[w] = solved[z, x, s] + factors[z, 2, pl.ds(w, 1)] * carried[w]
                solved[z, x, s] = carried[w]

    def coarse(read):
        layer_rows = inv_all.shape[0] * inv_all.shape[1]
        values = jnp.zeros((K, layer_rows), F32)
        for layer in range(n_slab):
            piece = inv_all[:, :, pl.ds(layer * aggregates, aggregates)]
            values = values + dot_nt(read(layer), piece.reshape(layer_rows, aggregates))
        return values

    def smooth(halo, values):
        for n, (d, x, s) in enumerate(rows):
            halo[d + 1, x + 1, s] = solved[slab * D + d, x, s] + dot_nn(values, onehot[n])

    def exchange(halo, phase):
        def sides():
            inner_x, inner_z = pl.ds(1, X), pl.ds(1, D)
            return (
                (slab > 0, (slab - 1, sub), halo.at[1, inner_x], halo.at[D + 1, inner_x]),
                (slab < n_slab - 1, (slab + 1, sub), halo.at[D, inner_x], halo.at[0, inner_x]),
                (sub > 0, (slab, sub - 1), halo.at[inner_z, 1], halo.at[inner_z, X + 1]),
                (sub < n_sub - 1, (slab, sub + 1), halo.at[inner_z, X], halo.at[inner_z, 0]),
            )

        for side, (present, target, source, place) in enumerate(sides()):
            @pl.when(present)
            def _(side=side, target=target, source=source, place=place):
                pltpu.make_async_remote_copy(
                    src_ref=source, dst_ref=place,
                    send_sem=halo_send.at[phase, side], recv_sem=halo_recv.at[phase, side],
                    device_id=target, device_id_type=MESH,
                ).start()

        for side, (present, target, source, place) in enumerate(sides()):
            landing = sides()[side ^ 1][3]

            @pl.when(present)
            def _(side=side, target=target, source=source, landing=landing):
                pltpu.make_async_remote_copy(
                    src_ref=source, dst_ref=landing,
                    send_sem=halo_send.at[phase, side], recv_sem=halo_recv.at[phase, side ^ 1],
                    device_id=target, device_id_type=MESH,
                ).wait()

    def apply_operator(halo, n):
        total = jnp.zeros((K, C), F32)
        d, x, s = rows[n]
        for slot in range(slots):
            number = pattern[n * slots + slot]
            remain = number % plane_blocks
            local_plane = jnp.clip(number // plane_blocks - slab * D + 1, 0, D + 1)
            local_cross = jnp.clip(remain // S - sub * X + 1, 0, X + 1)
            total = total + dot_nt(halo[local_plane, local_cross, remain % S], blocks[d, x, s, slot])
        return total

    lane = lax.broadcasted_iota(jnp.int32, (K, C), 1)
    place = lax.broadcasted_iota(jnp.int32, (K, C), 0)

    def to_row(first, second):
        first = jnp.sum(first, axis=1, keepdims=True)
        second = jnp.sum(second, axis=1, keepdims=True)
        spread = jnp.where(lane == place, first, 0.0) + jnp.where(lane == place + K, second, 0.0)
        return jnp.sum(spread, axis=0, keepdims=True)

    def from_row(row):
        first = jnp.sum(jnp.where(lane == place, row, 0.0), axis=1, keepdims=True)
        second = jnp.sum(jnp.where(lane == place + K, row, 0.0), axis=1, keepdims=True)
        return first, second

    lines_wait()
    line_solve(lambda block, d, x, s: lines_r[block, d, x, s])
    slab_wait()
    inv_wait()
    smooth(halo_0, coarse(lambda layer: slab_a[layer]))

    exchange(halo_0, 0)
    energy = jnp.zeros((K, C), F32)
    curvature = jnp.zeros((K, C), F32)
    for n, (d, x, s) in enumerate(rows):
        applied = apply_operator(halo_0, n)
        lines_w[slab, d, x, s] = applied
        applied_0[d, x, s] = applied
        smoothed = halo_0[d + 1, x + 1, s]
        energy = energy + rhs[d, x, s] * smoothed
        curvature = curvature + applied * smoothed

    sub_c[sub, pl.ds(0, K)] = local_sums(lambda d, x, s: applied_0[d, x, s])
    sub_c[sub, pl.ds(K, 1)] = to_row(energy, curvature)
    sums_wait = copies("sub", sub_c, sub_send.at[1], sub_recv.at[1])
    lines_wait = copies("slab", lines_w, line_send.at[1], line_recv.at[1])
    sums_wait()
    total = sub_c[0]
    for other in range(1, n_sub):
        total = total + sub_c[other]
    slab_c[slab] = total
    slab_wait = copies("slab", slab_c, slab_send.at[1], slab_recv.at[1])
    slab_wait()
    row = slab_c[0, pl.ds(K, 1)]
    for other in range(1, n_slab):
        row = row + slab_c[other, pl.ds(K, 1)]
    energy, curvature = from_row(row)
    step_length = energy / curvature
    values = coarse(lambda layer: slab_a[layer] - step_length * slab_c[layer, pl.ds(0, K)])
    lines_wait()
    line_solve(
        lambda block, d, x, s: lines_r[block, d, x, s] - step_length * lines_w[block, d, x, s]
    )
    smooth(halo_1, values)

    exchange(halo_1, 1)
    energy_sum = jnp.zeros((K, C), F32)
    curvature_sum = jnp.zeros((K, C), F32)
    for n, (d, x, s) in enumerate(rows):
        applied = apply_operator(halo_1, n)
        sol[d, x, s] = applied
        smoothed = halo_1[d + 1, x + 1, s]
        residual = rhs[d, x, s] - step_length * applied_0[d, x, s]
        energy_sum = energy_sum + residual * smoothed
        curvature_sum = curvature_sum + applied * smoothed

    sub_e[sub] = to_row(energy_sum, curvature_sum)
    copies("sub", sub_e, sub_send.at[2], sub_recv.at[2])()
    row = sub_e[0]
    for other in range(1, n_sub):
        row = row + sub_e[other]
    slab_e[slab] = row
    copies("slab", slab_e, slab_send.at[2], slab_recv.at[2])()
    row = slab_e[0]
    for other in range(1, n_slab):
        row = row + slab_e[other]
    energy_next, curvature = from_row(row)
    growth = energy_next / energy
    step_next = energy_next / (curvature - growth * energy_next / step_length)
    for n, (d, x, s) in enumerate(rows):
        first, second = halo_0[d + 1, x + 1, s], halo_1[d + 1, x + 1, s]
        along_0, along_1 = applied_0[d, x, s], sol[d, x, s]
        residual = rhs[d, x, s] - step_length * along_0
        res[d, x, s] = residual - step_next * (along_1 + growth * along_0)
        sol[d, x, s] = step_length * first + step_next * (second + growth * first)


def per_device(n_slab, n_sub, right_side, blocks, pattern, aggregates, coarse_inverse):
    D, X, S, K, C = right_side.shape
    owned, everything = coarse_inverse.shape
    layer = owned * n_sub
    planes = n_slab * D
    packed = -(-(K + 1) // 8) * 8
    rows = D * X * S
    field = (D, X, S, K, C)
    halo = (D + 2, X + 2, S, K, C)
    dma = pltpu.SemaphoreType.DMA
    vmem = pl.BlockSpec(memory_space=pltpu.VMEM)
    return pl.pallas_call(
        functools.partial(kernel, n_slab, n_sub),
        out_shape=[jax.ShapeDtypeStruct(field, F32)] * 2,
        in_specs=[pl.BlockSpec(memory_space=pltpu.SMEM), vmem, vmem, vmem, vmem],
        out_specs=[vmem, vmem],
        scratch_shapes=[
            pltpu.VMEM((n_slab,) + field, F32),
            pltpu.VMEM((n_slab,) + field, F32),
            pltpu.VMEM((n_slab, 2 * rows, C), F32),
            pltpu.VMEM((planes, 3, X * S, C), F32),
            pltpu.VMEM((planes, X, S, K, C), F32),
            pltpu.VMEM((n_sub, K, layer), F32),
            pltpu.VMEM((n_sub, packed, layer), F32),
            pltpu.VMEM((n_sub, 1, C), F32),
            pltpu.VMEM((n_slab, K, layer), F32),
            pltpu.VMEM((n_slab, packed, layer), F32),
            pltpu.VMEM((n_slab, 1, C), F32),
            pltpu.VMEM((n_sub, owned, everything), F32),
            pltpu.VMEM(halo, F32),
            pltpu.VMEM(halo, F32),
            pltpu.VMEM(field, F32),
            pltpu.VMEM((rows, layer, C), F32),
            dma((2, n_slab)), dma((2, n_slab)),
            dma((n_slab,)), dma((n_slab,)),
            dma((n_sub,)), dma((n_sub,)),
            dma((3, n_sub)), dma((3, n_sub)),
            dma((3, n_slab)), dma((3, n_slab)),
            dma((2, 4)), dma((2, 4)),
        ],
        compiler_params=pltpu.CompilerParams(
            collective_id=0, has_side_effects=True, vmem_limit_bytes=60 * 1024 * 1024
        ),
        name="whole_solve",
    )(pattern.reshape(-1), right_side, blocks, aggregates, coarse_inverse)


def solution(mesh):
    placed = (
        P("slab", "sub", None, None, None),
        P("slab", "sub", None, None, None, None),
        P("slab", "sub", None, None),
        P("slab", "sub", None, None),
        P(("slab", "sub"), None),
    )
    body = functools.partial(per_device, mesh.shape["slab"], mesh.shape["sub"])
    return jax.shard_map(
        lambda *args: tuple(body(*args)),
        mesh=mesh,
        in_specs=placed,
        out_specs=(P("slab", "sub", None, None, None), P("slab", "sub", None, None, None)),
        check_vma=False,
    )
```

time: 468 us -> 57.3 us (0.12)
  blocking collectives: 395 us -> 0 us
  Pallas kernels: 0 us -> 51.1 us
  local copies, waits for them, and re-layouts: 29.3 us -> 3.86 us
  starting transfers between devices: 15.5 us -> 0 us
  waiting for transfers between devices: 15.1 us -> 0 us
  matrix products: 4.95 us -> 0 us
    all_gather x14 -> x0, blocking collectives: 303 us -> none  [the longest x10 231 us: prefix_2(): pieces = jax.tree.map(lambda part: lax.all_gather(part, axis), value)]
    psum x4 -> x0, blocking collectives: 92.3 us -> none  [the longest x2 80.3 us: paired(): lax.psum((local_inner(vector_r, vector_z), local_inner(vector_w, vector_z...]
    pallas_call x0 -> x1, Pallas kernels: none -> 51.1 us  [per_device(): pl.pallas_call(functools.partial(kernel, n_slab, n_sub), out_shape=[jax.S...]
    unnamed x15 -> x3, local copies, waits for them, and re-layouts: 25.4 us -> 3.26 us
    ppermute x9 -> x0, starting transfers between devices: 15.5 us -> none  [the longest x4 9.05 us: padded_2(): before = lax.ppermute(last, axis, up)]
    ppermute x9 -> x0, waiting for transfers between devices: 15.1 us -> none  [the longest x4 14.9 us: padded_2(): after = lax.ppermute(leading, axis, down)]
    dot_general x8 -> x0, matrix products: 4.95 us -> none  [the longest x2 3.83 us: operator_apply(): jnp.einsum('rsij,rskj->rki', flat_blocks, nearby, precision=HIGHEST, pref...]
  transfers between devices with their start and end apart: 9 -> 0, of which waited for: 5 -> 0; matrix products, arithmetic and copies ran while one was open for 0% -> 0% of each run, Pallas kernels for 0% -> 0%
where the time goes in v1:
time: 57.3 us; the launch traced here: 57 us
  Pallas kernels  51.1 us (89%)
  local copies, waits for them, and re-layouts  3.86 us (7%)
  other arithmetic  1.34 us (2%)
  between operations  0.64 us (1%)
    pallas_call x1, Pallas kernels, per_device(): pl.pallas_call(functools.partial(kernel, n_slab, n_sub), out_shape=[jax.S...  51.1 us
    unnamed x3, local copies, waits for them, and re-layouts  3.26 us
    unnamed x1, other arithmetic  1.34 us

profile of v1, /device:TPU:0, one launch (start us, length us, event | category | flops | bytes accessed | tf_op | source)
XLA Modules:
  0.0 57.0 jit_solution(17425369769305370508)
XLA Ops:
  0.6 0.5 broadcast.3
  1.1 1.3 %reduce.3 = s32[2,2,7]{2,1,0:T(2,128)S(1)} reduce(s32[2,2,1,7]{3,2,1,0:T(1,128)} %param.7, s32[]{:T(128)} %broadcast.3), dimensions={2}, to_apply=%param.7.reduce_sub_computation.3 | reduce | bytes 228 | tf_op args[2]
  2.5 0.6 %reshape.7.pattern = s32[28]{0:T(128)} reshape(s32[2,2,7]{2,1,0:T(2,128)S(1)} %reduce.3) | data formatting | bytes 224 | tf_op jit(solution)/shard_map/reshape | solution.py:346
  3.1 51.1 %whole_solve.1 = (f32[2,2,1,16,128]{4,3,2,1,0:T(8,128)}, f32[2,2,1,16,128]{4,3,2,1,0:T(8,128)}) custom-call(s32[28]{0:T(128)} %reshape.7.pattern, f32[2,2,1,16,128]{4,3,2,1,0:T(8,128)} %rhs.5, f32[2,2,1,7,128,128]{5,4,3,2,1,0:T(8,128)} %blocks.1, s32[2,2,1,128]{3,2,1,0:T(1,128)} %agg.1, f32[32,1024]{1,0:T(8,128)} %inverse.1), custom_call_target="tpu_custom_call" | custom-call | tf_op jit(solution)/shard_map/whole_solve/pallas_call | solution.py:313
  54.2 1.4 %copy.9 = f32[2,2,1,16,128]{4,3,2,1,0:T(8,128)} copy(f32[2,2,1,16,128]{4,3,2,1,0:T(8,128)} %get-tuple-element.4) | data formatting | bytes 65536
  55.6 1.4 %copy.10 = f32[2,2,1,16,128]{4,3,2,1,0:T(8,128)} copy(f32[2,2,1,16,128]{4,3,2,1,0:T(8,128)} %get-tuple-element.5) | data formatting | bytes 65536

commit v2 on v1

--- a/solution.py
+++ b/solution.py
@@ -6,31 +6,49 @@
 from jax.experimental.pallas import tpu as pltpu
 from jax.sharding import PartitionSpec as P
 
-HIGHEST = lax.Precision.HIGHEST
 MESH = pl.DeviceIdType.MESH
 F32 = jnp.float32
-
-
-def dot_nt(left, right):
+BF16 = jnp.bfloat16
+
+
+def dot(left, right, right_dim):
     return lax.dot_general(
-        left, right, (((1,), (1,)), ((), ())), precision=HIGHEST, preferred_element_type=F32
+        left, right, (((1,), (right_dim,)), ((), ())), preferred_element_type=F32
     )
 
 
-def dot_nn(left, right):
-    return lax.dot_general(
-        left, right, (((1,), (0,)), ((), ())), precision=HIGHEST, preferred_element_type=F32
-    )
+def pieces(value, count, axis=0):
+    parts = []
+    for _ in range(count):
+        part = value.astype(BF16)
+        parts.append(part)
+        value = value - part.astype(F32)
+    return jnp.concatenate(parts, axis=axis)
+
+
+def joined(product):
+    height, half = product.shape[0] // 3, product.shape[1] // 2
+    high, mid, low = (product[n * height : (n + 1) * height] for n in range(3))
+    small = low[:, :half] + mid[:, half:] + low[:, half:]
+    return small + (mid[:, :half] + high[:, half:]) + high[:, :half]
+
+
+def stacked(product):
+    height = product.shape[0] // 3
+    return (product[2 * height :] + product[height : 2 * height]) + product[:height]
 
 
 def kernel(
     n_slab, n_sub, pattern, rhs, blocks, agg, inverse, sol, res,
     lines_r, lines_w, coefs, factors, solved, sub_a, sub_c, sub_e, slab_a, slab_c, slab_e,
     inv_all, halo_0, halo_1, applied_0, onehot,
+    block_here, block_split, inv_split, halo_split, block_sem,
     line_send, line_recv, coef_send, coef_recv, inv_send, inv_recv,
     sub_send, sub_recv, slab_send, slab_recv, halo_send, halo_recv,
 ):
     D, X, S, K, C = rhs.shape
+    block_copy = pltpu.make_async_copy(blocks, block_here, block_sem)
+    block_copy.start()
     slots = blocks.shape[3]
     aggregates = inv_all.shape[0] * inv_all.shape[1]
     slab, sub = lax.axis_index("slab"), lax.axis_index("sub")
@@ -85,13 +103,11 @@
 
     a_index = lax.broadcasted_iota(jnp.int32, (aggregates, C), 0)
     for n, (d, x, s) in enumerate(rows):
-        onehot[n] = (agg[d, x, s][None, :] == a_index).astype(F32)
+        onehot[:, pl.ds(n * C, C)] = (agg[d, x, s][None, :] == a_index).astype(F32).astype(BF16)
 
     def local_sums(read):
-        total = jnp.zeros((K, aggregates), F32)
-        for n, (d, x, s) in enumerate(rows):
-            total = total + dot_nt(read(d, x, s), onehot[n])
-        return total
+        split = jnp.concatenate([pieces(read(d, x, s), 3) for d, x, s in rows], axis=1)
+        return stacked(dot(split, onehot[...], 1))
 
     sub_a[sub] = local_sums(lambda d, x, s: rhs[d, x, s])
     lines_r[slab] = rhs[...]
@@ -99,6 +115,7 @@
 
     global_cross = X * n_sub
     plane_blocks = global_cross * S
+    block_copy.wait()
     eye = (
         lax.broadcasted_iota(jnp.int32, (C, C), 0) == lax.broadcasted_iota(jnp.int32, (C, C), 1)
     ).astype(F32)
@@ -107,8 +124,8 @@
         diagonal = jnp.zeros((C, C), F32)
         coupling = jnp.zeros((C, C), F32)
         for slot in range(slots):
-            number = pattern[n * slots + slot]
-            block = blocks[d, x, s, slot]
+            number = pattern[d, x, s, slot]
+            block = block_here[d, x, s, slot]
             diagonal = diagonal + (number == own).astype(F32) * block
             coupling = coupling + (number == own - plane_blocks).astype(F32) * block
         coefs[slab, pl.ds(n, 1)] = jnp.sum(diagonal * eye, axis=0, keepdims=True)
@@ -146,11 +163,11 @@
         if z + 1 < planes:
             factors[z, 2] = -coef(1, z + 1) * inverse_pivot
 
-    def line_solve(read):
+    def line_solve(lines):
         carried = [None] * width
         for z in range(planes):
             for w, (x, s) in enumerate(cells):
-                value = read(z // D, z % D, x, s) * factors[z, 0, pl.ds(w, 1)]
+                value = lines[z // D, z % D, x, s] * factors[z, 0, pl.ds(w, 1)]
                 if z > 0:
                     value = value + factors[z, 1, pl.ds(w, 1)] * carried[w]
                 carried[w] = value
@@ -161,16 +178,13 @@
                 solved[z, x, s] = carried[w]
 
     def coarse(read):
-        layer_rows = inv_all.shape[0] * inv_all.shape[1]
-        values = jnp.zeros((K, layer_rows), F32)
-        for layer in range(n_slab):
-            piece = inv_all[:, :, pl.ds(layer * aggregates, aggregates)]
-            values = values + dot_nt(read(layer), piece.reshape(layer_rows, aggregates))
-        return values
-
-    def smooth(halo, values):
-        for n, (d, x, s) in enumerate(rows):
-            halo[d + 1, x + 1, s] = solved[slab * D + d, x, s] + dot_nn(values, onehot[n])
+        split = jnp.concatenate([pieces(read(layer), 3) for layer in range(n_slab)], axis=1)
+        values = joined(dot(split, inv_split[...], 1))
+        return stacked(dot(pieces(values, 3), onehot[...], 0))
+
+    for n, (d, x, s) in enumerate(rows):
+        for slot in range(slots):
+            block_split[n, :, pl.ds(slot * C, C)] = pieces(block_here[d, x, s, slot], 2)
 
     def exchange(halo, phase):
         def sides():
@@ -202,16 +216,23 @@
                     device_id=target, device_id_type=MESH,
                 ).wait()
 
-    def apply_operator(halo, n):
-        total = jnp.zeros((K, C), F32)
+    def split_halo(halo):
+        for d in range(D + 2):
+            for x in range(X + 2):
+                if 0 < d <= D or 0 < x <= X:
+                    for s in range(S):
+                        halo_split[d, x, s] = pieces(halo[d, x, s], 3)
+
+    def apply_operator(n):
         d, x, s = rows[n]
+        nearby = []
         for slot in range(slots):
-            number = pattern[n * slots + slot]
+            number = pattern[d, x, s, slot]
             remain = number % plane_blocks
             local_plane = jnp.clip(number // plane_blocks - slab * D + 1, 0, D + 1)
             local_cross = jnp.clip(remain // S - sub * X + 1, 0, X + 1)
-            total = total + dot_nt(halo[local_plane, local_cross, remain % S], blocks[d, x, s, slot])
-        return total
+            nearby.append(halo_split[local_plane, local_cross, remain % S])
+        return joined(dot(jnp.concatenate(nearby, axis=1), block_split[n], 1))
 
     lane = lax.broadcasted_iota(jnp.int32, (K, C), 1)
     place = lax.broadcasted_iota(jnp.int32, (K, C), 0)
@@ -227,17 +248,26 @@
         second = jnp.sum(jnp.where(lane == place + K, row, 0.0), axis=1, keepdims=True)
         return first, second
 
+    inv_wait()
+    for other in range(n_sub):
+        owned = inv_all.shape[1]
+        part = inv_all[other]
+        high = part.astype(BF16)
+        inv_split[pl.ds(other * owned, owned)] = high
+        inv_split[pl.ds((n_sub + other) * owned, owned)] = (part - high.astype(F32)).astype(BF16)
     lines_wait()
-    line_solve(lambda block, d, x, s: lines_r[block, d, x, s])
+    line_solve(lines_r)
     slab_wait()
-    inv_wait()
-    smooth(halo_0, coarse(lambda layer: slab_a[layer]))
+    spread = coarse(lambda layer: slab_a[layer])
+    for n, (d, x, s) in enumerate(rows):
+        halo_0[d + 1, x + 1, s] = solved[slab * D + d, x, s] + spread[:, n * C : (n + 1) * C]
 
     exchange(halo_0, 0)
+    split_halo(halo_0)
     energy = jnp.zeros((K, C), F32)
     curvature = jnp.zeros((K, C), F32)
     for n, (d, x, s) in enumerate(rows):
-        applied = apply_operator(halo_0, n)
+        applied = apply_operator(n)
         lines_w[slab, d, x, s] = applied
         applied_0[d, x, s] = applied
         smoothed = halo_0[d + 1, x + 1, s]
@@ -254,24 +284,25 @@
         total = total + sub_c[other]
     slab_c[slab] = total
     slab_wait = copies("slab", slab_c, slab_send.at[1], slab_recv.at[1])
+    lines_wait()
+    line_solve(lines_w)
     slab_wait()
     row = slab_c[0, pl.ds(K, 1)]
     for other in range(1, n_slab):
         row = row + slab_c[other, pl.ds(K, 1)]
     energy, curvature = from_row(row)
     step_length = energy / curvature
-    values = coarse(lambda layer: slab_a[layer] - step_length * slab_c[layer, pl.ds(0, K)])
-    lines_wait()
-    line_solve(
-        lambda block, d, x, s: lines_r[block, d, x, s] - step_length * lines_w[block, d, x, s]
-    )
-    smooth(halo_1, values)
+    spread = coarse(lambda layer: slab_c[layer, pl.ds(0, K)])
+    for n, (d, x, s) in enumerate(rows):
+        change = solved[slab * D + d, x, s] + spread[:, n * C : (n + 1) * C]
+        halo_1[d + 1, x + 1, s] = halo_0[d + 1, x + 1, s] - step_length * change
 
     exchange(halo_1, 1)
+    split_halo(halo_1)
     energy_sum = jnp.zeros((K, C), F32)
     curvature_sum = jnp.zeros((K, C), F32)
     for n, (d, x, s) in enumerate(rows):
-        applied = apply_operator(halo_1, n)
+        applied = apply_operator(n)
         sol[d, x, s] = applied
         smoothed = halo_1[d + 1, x + 1, s]
         residual = rhs[d, x, s] - step_length * applied_0[d, x, s]
@@ -313,7 +344,9 @@
     return pl.pallas_call(
         functools.partial(kernel, n_slab, n_sub),
         out_shape=[jax.ShapeDtypeStruct(field, F32)] * 2,
-        in_specs=[pl.BlockSpec(memory_space=pltpu.SMEM), vmem, vmem, vmem, vmem],
+        in_specs=[
+            pl.BlockSpec(memory_space=pltpu.SMEM), vmem, pl.BlockSpec(memory_space=pl.ANY), vmem, vmem,
+        ],
         out_specs=[vmem, vmem],
         scratch_shapes=[
             pltpu.VMEM((n_slab,) + field, F32),
@@ -331,7 +364,12 @@
             pltpu.VMEM(halo, F32),
             pltpu.VMEM(halo, F32),
             pltpu.VMEM(field, F32),
-            pltpu.VMEM((rows, layer, C), F32),
+            pltpu.VMEM((layer, rows * C), BF16),
+            pltpu.VMEM(blocks.shape, F32),
+            pltpu.VMEM((rows, 2 * C, blocks.shape[3] * C), BF16),
+            pltpu.VMEM((2 * layer, everything), BF16),
+            pltpu.VMEM((D + 2, X + 2, S, 3 * K, C), BF16),
+            dma,
             dma((2, n_slab)), dma((2, n_slab)),
             dma((n_slab,)), dma((n_slab,)),
             dma((n_sub,)), dma((n_sub,)),
@@ -343,7 +381,7 @@
             collective_id=0, has_side_effects=True, vmem_limit_bytes=60 * 1024 * 1024
         ),
         name="whole_solve",
-    )(pattern.reshape(-1), right_side, blocks, aggregates, coarse_inverse)
+    )(pattern, right_side, blocks, aggregates, coarse_inverse)
 
 
 def solution(mesh):

time: 57.3 us -> 45.5 us (0.79)
  Pallas kernels: 51.1 us -> 41.8 us
  other arithmetic: 1.34 us -> 0 us
  local copies, waits for them, and re-layouts: 3.86 us -> 2.75 us
    pallas_call x1, Pallas kernels: 51.1 us -> 41.8 us  [per_device(): pl.pallas_call(functools.partial(kernel, n_slab, n_sub), out_shape=[jax.S...]
    unnamed x1 -> x0, other arithmetic: 1.34 us -> none
    reshape x1 -> x0, local copies, waits for them, and re-layouts: 0.6 us -> none  [per_device(): pattern.reshape(-1)]
    unnamed x3 -> x2, local copies, waits for them, and re-layouts: 3.26 us -> 2.75 us
where the time goes in v2:
time: 45.5 us; the launch traced here: 45.2 us
  Pallas kernels  41.8 us (92%)
  local copies, waits for them, and re-layouts  2.75 us (6%)
  between operations  0.64 us (1%)
    pallas_call x1, Pallas kernels, per_device(): pl.pallas_call(functools.partial(kernel, n_slab, n_sub), out_shape=[jax.S...  41.8 us
    unnamed x2, local copies, waits for them, and re-layouts  2.75 us

profile of v2, /device:TPU:0, one launch (start us, length us, event | category | flops | bytes accessed | tf_op | source)
XLA Modules:
  0.0 45.2 jit_solution(7545699448473768535)
XLA Ops:
  0.6 41.8 %whole_solve.1 = (f32[2,2,1,16,128]{4,3,2,1,0:T(8,128)}, f32[2,2,1,16,128]{4,3,2,1,0:T(8,128)}) custom-call(s32[2,2,1,7]{3,2,1,0:T(1,128)} %pattern.1, f32[2,2,1,16,128]{4,3,2,1,0:T(8,128)} %rhs.1, f32[2,2,1,7,128,128]{5,4,3,2,1,0:T(8,128)} %blocks.1, s32[2,2,1,128]{3,2,1,0:T(1,128)} %agg.1, f32[32,1024]{1,0:T(8,128)} %inverse.1), custom_call_target="tpu_custom_call" | custom-call | tf_op jit(solution)/shard_map/whole_solve/pallas_call | solution.py:344
  42.5 1.4 %copy.9 = f32[2,2,1,16,128]{4,3,2,1,0:T(8,128)} copy(f32[2,2,1,16,128]{4,3,2,1,0:T(8,128)} %get-tuple-element.4) | data formatting | bytes 65536
  43.8 1.4 %copy.10 = f32[2,2,1,16,128]{4,3,2,1,0:T(8,128)} copy(f32[2,2,1,16,128]{4,3,2,1,0:T(8,128)} %get-tuple-element.5) | data formatting | bytes 65536

commit v3 on v2

--- a/solution.py
+++ b/solution.py
@@ -109,7 +109,7 @@
         split = jnp.concatenate([pieces(read(d, x, s), 3) for d, x, s in rows], axis=1)
         return stacked(dot(split, onehot[...], 1))
 
-    sub_a[sub] = local_sums(lambda d, x, s: rhs[d, x, s])
+    slab_a[slab] = local_sums(lambda d, x, s: rhs[d, x, s])
     lines_r[slab] = rhs[...]
     inv_all[sub] = inverse[...]
 
@@ -133,17 +133,35 @@
 
     pl.semaphore_wait(barrier, n_slab + n_sub - 2)
 
-    sums_wait = copies("sub", sub_a, sub_send.at[0], sub_recv.at[0])
+    slab_wait = copies("slab", slab_a, slab_send.at[0], slab_recv.at[0])
     coefs_wait = copies("slab", coefs, coef_send, coef_recv)
+    inv_wait = copies("sub", inv_all, inv_send, inv_recv, inverse)
     lines_wait = copies("slab", lines_r, line_send.at[0], line_recv.at[0], rhs)
-    inv_wait = copies("sub", inv_all, inv_send, inv_recv, inverse)
-
-    sums_wait()
-    total = sub_a[0]
-    for other in range(1, n_sub):
-        total = total + sub_a[other]
-    slab_a[slab] = total
-    slab_wait = copies("slab", slab_a, slab_send.at[0], slab_recv.at[0])
+
+    inv_wait()
+    for other in range(n_sub):
+        owned = inv_all.shape[1]
+        part = inv_all[other]
+        high = part.astype(BF16)
+        inv_split[pl.ds(other * owned, owned)] = high
+        inv_split[pl.ds((n_sub + other) * owned, owned)] = (part - high.astype(F32)).astype(BF16)
+
+    def coarse_part(read):
+        split = jnp.concatenate([pieces(read(layer), 3) for layer in range(n_slab)], axis=1)
+        return joined(dot(split, inv_split[...], 1))
+
+    def coarse_spread(values):
+        return stacked(dot(pieces(values, 3), onehot[...], 0))
+
+    def summed(buffer, count):
+        total = buffer[0]
+        for other in range(1, count):
+            total = total + buffer[other]
+        return total
+
+    slab_wait()
+    sub_a[sub] = coarse_part(lambda layer: slab_a[layer])
+    sub_wait = copies("sub", sub_a, sub_send.at[0], sub_recv.at[0])
 
     coefs_wait()
     planes = n_slab * D
@@ -177,11 +195,6 @@
                 carried[w] = solved[z, x, s] + factors[z, 2, pl.ds(w, 1)] * carried[w]
                 solved[z, x, s] = carried[w]
 
-    def coarse(read):
-        split = jnp.concatenate([pieces(read(layer), 3) for layer in range(n_slab)], axis=1)
-        values = joined(dot(split, inv_split[...], 1))
-        return stacked(dot(pieces(values, 3), onehot[...], 0))
-
     for n, (d, x, s) in enumerate(rows):
         for slot in range(slots):
             block_split[n, :, pl.ds(slot * C, C)] = pieces(block_here[d, x, s, slot], 2)
@@ -248,17 +261,10 @@
         second = jnp.sum(jnp.where(lane == place + K, row, 0.0), axis=1, keepdims=True)
         return first, second
 
-    inv_wait()
-    for other in range(n_sub):
-        owned = inv_all.shape[1]
-        part = inv_all[other]
-        high = part.astype(BF16)
-        inv_split[pl.ds(other * owned, owned)] = high
-        inv_split[pl.ds((n_sub + other) * owned, owned)] = (part - high.astype(F32)).astype(BF16)
     lines_wait()
     line_solve(lines_r)
-    slab_wait()
-    spread = coarse(lambda layer: slab_a[layer])
+    sub_wait()
+    spread = coarse_spread(summed(sub_a, n_sub))
     for n, (d, x, s) in enumerate(rows):
         halo_0[d + 1, x + 1, s] = solved[slab * D + d, x, s] + spread[:, n * C : (n + 1) * C]
 
@@ -274,25 +280,24 @@
         energy = energy + rhs[d, x, s] * smoothed
         curvature = curvature + applied * smoothed
 
-    sub_c[sub, pl.ds(0, K)] = local_sums(lambda d, x, s: applied_0[d, x, s])
-    sub_c[sub, pl.ds(K, 1)] = to_row(energy, curvature)
-    sums_wait = copies("sub", sub_c, sub_send.at[1], sub_recv.at[1])
+    slab_c[slab, pl.ds(0, K)] = local_sums(lambda d, x, s: applied_0[d, x, s])
+    slab_c[slab, pl.ds(K, 1)] = to_row(energy, curvature)
+    slab_wait = copies("slab", slab_c, slab_send.at[1], slab_recv.at[1])
     lines_wait = copies("slab", lines_w, line_send.at[1], line_recv.at[1])
-    sums_wait()
-    total = sub_c[0]
-    for other in range(1, n_sub):
-        total = total + sub_c[other]
-    slab_c[slab] = total
-    slab_wait = copies("slab", slab_c, slab_send.at[1], slab_recv.at[1])
-    lines_wait()
-    line_solve(lines_w)
     slab_wait()
     row = slab_c[0, pl.ds(K, 1)]
     for other in range(1, n_slab):
         row = row + slab_c[other, pl.ds(K, 1)]
-    energy, curvature = from_row(row)
+    sub_c[sub, pl.ds(K, 1)] = row
+    sub_c[sub, pl.ds(0, K)] = coarse_part(lambda layer: slab_c[layer, pl.ds(0, K)])
+    sub_wait = copies("sub", sub_c, sub_send.at[1], sub_recv.at[1])
+    lines_wait()
+    line_solve(lines_w)
+    sub_wait()
+    total = summed(sub_c, n_sub)
+    energy, curvature = from_row(total[K : K + 1])
     step_length = energy / curvature
-    spread = coarse(lambda layer: slab_c[layer, pl.ds(0, K)])
+    spread = coarse_spread(total[:K])
     for n, (d, x, s) in enumerate(rows):
         change = solved[slab * D + d, x, s] + spread[:, n * C : (n + 1) * C]
         halo_1[d + 1, x + 1, s] = halo_0[d + 1, x + 1, s] - step_length * change
@@ -330,6 +335,11 @@
         sol[d, x, s] = step_length * first + step_next * (second + growth * first)
 
 
+def hand_over(first_in, second_in, first_out, second_out):
+    first_out[...] = first_in[...]
+    second_out[...] = second_in[...]
+
+
 def per_device(n_slab, n_sub, right_side, blocks, pattern, aggregates, coarse_inverse):
     D, X, S, K, C = right_side.shape
     owned, everything = coarse_inverse.shape
@@ -341,7 +351,7 @@
     halo = (D + 2, X + 2, S, K, C)
     dma = pltpu.SemaphoreType.DMA
     vmem = pl.BlockSpec(memory_space=pltpu.VMEM)
-    return pl.pallas_call(
+    outputs = pl.pallas_call(
         functools.partial(kernel, n_slab, n_sub),
         out_shape=[jax.ShapeDtypeStruct(field, F32)] * 2,
         in_specs=[
@@ -382,6 +392,14 @@
         ),
         name="whole_solve",
     )(pattern, right_side, blocks, aggregates, coarse_inverse)
+    return pl.pallas_call(
+        hand_over,
+        out_shape=[jax.ShapeDtypeStruct(field, F32)] * 2,
+        in_specs=[vmem, vmem],
+        out_specs=[vmem, vmem],
+        compiler_params=pltpu.CompilerParams(vmem_limit_bytes=1024 * 1024),
+        name="hand_over",
+    )(*outputs)
 
 
 def solution(mesh):

time: 45.5 us -> 45.4 us (level)
  local copies, waits for them, and re-layouts: 2.75 us -> 1.51 us
  Pallas kernels: 41.8 us -> 43 us
    unnamed x2 -> x4, local copies, waits for them, and re-layouts: 2.75 us -> 1.51 us
    pallas_call x0 -> x1, Pallas kernels: none -> 0.63 us  [per_device(): pl.pallas_call(hand_over, out_shape=[jax.ShapeDtypeStruct(field, F32)] *...]
    pallas_call x1, Pallas kernels: 41.8 us -> 42.4 us  [per_device(): pl.pallas_call(functools.partial(kernel, n_slab, n_sub), out_shape=[jax.S...]
where the time goes in v3:
time: 45.4 us; the launch traced here: 45.1 us
  Pallas kernels  43 us (95%)
  local copies, waits for them, and re-layouts  1.51 us (3%)
  between operations  0.65 us (1%)
    pallas_call x1, Pallas kernels, per_device(): pl.pallas_call(functools.partial(kernel, n_slab, n_sub), out_shape=[jax.S...  42.4 us
    unnamed x4, local copies, waits for them, and re-layouts  1.51 us

profile of v3, /device:TPU:0, one launch (start us, length us, event | category | flops | bytes accessed | tf_op | source)
XLA Modules:
  0.0 45.1 jit_solution(4089717148449723894)
XLA Ops:
  0.6 42.4 %whole_solve.1 = (f32[2,2,1,16,128]{4,3,2,1,0:T(8,128)}, f32[2,2,1,16,128]{4,3,2,1,0:T(8,128)}) custom-call(s32[2,2,1,7]{3,2,1,0:T(1,128)} %pattern.1, f32[2,2,1,16,128]{4,3,2,1,0:T(8,128)} %rhs.1, f32[2,2,1,7,128,128]{5,4,3,2,1,0:T(8,128)} %blocks.1, s32[2,2,1,128]{3,2,1,0:T(1,128)} %agg.1, f32[32,1024]{1,0:T(8,128)} %inverse.1), custom_call_target="tpu_custom_call" | custom-call | tf_op jit(solution)/shard_map/whole_solve/pallas_call | solution.py:354
  43.0 0.0 copy-start
  43.0 0.7 %copy-done = f32[2,2,1,16,128]{4,3,2,1,0:T(8,128)S(1)} copy-done((f32[2,2,1,16,128]{4,3,2,1,0:T(8,128)S(1)}, f32[2,2,1,16,128]{4,3,2,1,0:T(8,128)}, u32[]{:S(2)}) %copy-start) | copy-done | bytes 32792
  43.8 0.0 copy-start.1
  43.8 0.8 %copy-done.1 = f32[2,2,1,16,128]{4,3,2,1,0:T(8,128)S(1)} copy-done((f32[2,2,1,16,128]{4,3,2,1,0:T(8,128)S(1)}, f32[2,2,1,16,128]{4,3,2,1,0:T(8,128)}, u32[]{:S(2)}) %copy-start.1) | copy-done | bytes 32792
  44.5 0.6 %hand_over.1 = (f32[2,2,1,16,128]{4,3,2,1,0:T(8,128)}, f32[2,2,1,16,128]{4,3,2,1,0:T(8,128)}) custom-call(f32[2,2,1,16,128]{4,3,2,1,0:T(8,128)S(1)} %copy-done, f32[2,2,1,16,128]{4,3,2,1,0:T(8,128)S(1)} %copy-done.1), custom_call_target="tpu_custom_call" | custom-call | tf_op jit(solution)/shard_map/hand_over/pallas_call | solution.py:395
Async XLA Ops:
  43.0 0.8 %copy-start = (f32[2,2,1,16,128]{4,3,2,1,0:T(8,128)S(1)}, f32[2,2,1,16,128]{4,3,2,1,0:T(8,128)}, u32[]{:S(2)}) copy-start(f32[2,2,1,16,128]{4,3,2,1,0:T(8,128)} %get-tuple-element.4.first_in) | copy-start | bytes 98308
  43.8 0.8 %copy-start.1 = (f32[2,2,1,16,128]{4,3,2,1,0:T(8,128)S(1)}, f32[2,2,1,16,128]{4,3,2,1,0:T(8,128)}, u32[]{:S(2)}) copy-start(f32[2,2,1,16,128]{4,3,2,1,0:T(8,128)} %get-tuple-element.5.second_in) | copy-start | bytes 98308
